TPU v7x, 32 devices: a whole 2x2x4 slice. The times are simulated.
32 devices in a mesh: dp: 8 (over z, x), feat: 4 (over y, core).
Axes of the slice: x: 2, y: 2, z: 4, core: 2. Of those that a mesh axis runs over, the one named last changes fastest.
Arguments:
- activations: bfloat16 [2048, 8192], P('dp', 'feat'), may hold values from -6 to 6
- cotangent: bfloat16 [2048, 1024], P('dp'), may hold values from -0.13183594 to 0.13183594
- weight: float32 [8192, 1024], P('feat'), may hold values from -0.0625 to 0.0625
- stats_old: float32 [4, 8, 4, 256, 256], P('feat', 'dp'), as said below
- owners: int32 [32, 4], replicated, may hold values from 0 to 7, as said below
- next_acts: bfloat16 [2048, 8192], P('dp', 'feat'), may hold values from -6 to 6
Outputs:
- weight_new: float32 [8192, 1024], P('feat')
- stats_new: float32 [4, 8, 4, 256, 256], P('feat', 'dp')
- next_out: bfloat16 [2048, 1024], P('dp', 'feat')
Inputs may be any that keep to these rules, and one draw needn't show every extreme that they name: `owners`: blocks are grouped by the index of feat that holds their rows (8192 / (256 * 4) row blocks a group); in every group each dp index owns at most 4 blocks, and some dp index owns exactly 4. `stats_old`: every slot holds a symmetric positive definite matrix; slots that no block maps to are not read.
All inputs are finite; a program needn't handle non-finite values.
Results may differ from a plain program's by a relative error of at most 0.02.
Values may be sent and summed in bfloat16 or wider, within the bound.
A program may use at most 128 MiB of HBM per device.

v0:
```python
import jax
import jax.numpy as jnp
from jax import lax
from jax.sharding import PartitionSpec as P

ITERS = 6
decay_rate = 0.9
step_rate = 0.01


def from_root(x, axis, root):
    mine = lax.axis_index(axis) == root
    return lax.psum(jnp.where(mine, x, jnp.zeros_like(x)), axis)


def newton_root(stats):
    width = stats.shape[0]
    identity = jnp.eye(width, dtype=jnp.float32)
    norm_value = jnp.sqrt(jnp.sum(stats * stats) + 1e-06)
    matrix = stats / norm_value
    iterate = identity
    for counter in range(ITERS):
        factor = (5.0 * identity - matrix) / 4.0
        factor_low = factor.astype(jnp.bfloat16)
        iterate = jnp.dot(
            iterate.astype(jnp.bfloat16), factor_low, preferred_element_type=jnp.float32
        )
        if counter + 1 < ITERS:
            square = jnp.dot(factor_low, factor_low, preferred_element_type=jnp.float32).astype(
                jnp.bfloat16
            )
            fourth = jnp.dot(square, square, preferred_element_type=jnp.float32).astype(
                jnp.bfloat16
            )
            matrix = jnp.dot(
                fourth, matrix.astype(jnp.bfloat16), preferred_element_type=jnp.float32
            )
    return iterate * norm_value ** (-0.25)


def update_stats(grad_block, old_stats):
    gram = (
        jnp.dot(grad_block, grad_block.T, preferred_element_type=jnp.float32) / grad_block.shape[0]
    )
    return decay_rate * old_stats + (1.0 - decay_rate) * gram


def block_at(matrix, block_id, col_blocks, width):
    row_start = block_id // col_blocks * width
    col_start = block_id % col_blocks * width
    return lax.dynamic_slice(matrix, (row_start, col_start), (width, width))


def body(activations, cotangent, weight, stats_old, owners, next_acts):
    width = stats_old.shape[-1]
    slots = stats_old.shape[2]
    rows_dev, columns = weight.shape
    row_blocks = rows_dev // width
    col_blocks = columns // width
    block_count = row_blocks * col_blocks
    partial_grad = jnp.einsum(
        "td,tc->dc", activations, cotangent, preferred_element_type=jnp.float32
    )
    summed = lax.psum(partial_grad, "dp")
    grad_low = summed.astype(jnp.bfloat16)
    feat_index = lax.axis_index("feat")
    data_index = lax.axis_index("dp")
    own_list = lax.dynamic_slice_in_dim(owners, feat_index * row_blocks, row_blocks, 0).reshape(
        block_count
    )
    is_mine = (own_list == data_index).astype(jnp.int32)
    slot_of = jnp.cumsum(is_mine) - is_mine
    block_ids = jnp.arange(block_count, dtype=jnp.int32)
    slot_pick = jnp.clip(slot_of, 0, slots - 1)
    stats_list = []
    renewed_list = []
    chosen_list = []
    for position in range(slots):
        picked = (is_mine == 1) & (slot_of == position)
        alive = jnp.any(picked)
        chosen = jnp.sum(jnp.where(picked, block_ids, 0))
        grad_block = block_at(grad_low, chosen, col_blocks, width)
        renewed = update_stats(grad_block, stats_old[0, 0, position])
        stats_list.append(jnp.where(alive, renewed, 0.0))
        renewed_list.append(renewed)
        chosen_list.append(chosen)
    root_list = [newton_root(renewed) for renewed in renewed_list]
    new_list = []
    fresh_list = []
    for root_matrix, chosen in zip(root_list, chosen_list):
        grad_block = block_at(grad_low, chosen, col_blocks, width)
        weight_block = block_at(weight, chosen, col_blocks, width)
        update = jnp.dot(
            root_matrix.astype(jnp.bfloat16), grad_block, preferred_element_type=jnp.float32
        )
        fresh_list.append(weight_block - step_rate * update)
    candidates = jnp.stack(fresh_list)
    for position in range(block_count):
        sending = lax.dynamic_index_in_dim(candidates, slot_pick[position], 0, keepdims=False)
        new_list.append(
            from_root(sending.astype(jnp.bfloat16), "dp", own_list[position]).astype(sending.dtype)
        )
    new_blocks = jnp.stack(new_list)
    weight_new = (
        new_blocks.reshape(row_blocks, col_blocks, width, width)
        .transpose(0, 2, 1, 3)
        .reshape(rows_dev, columns)
    )
    stats_out = jnp.stack(stats_list)[None, None]
    partial_next = jnp.dot(
        next_acts, weight_new.astype(jnp.bfloat16), preferred_element_type=jnp.float32
    )
    next_out = lax.psum_scatter(
        partial_next.astype(jnp.bfloat16), "feat", scatter_dimension=1, tiled=True
    )
    return (weight_new, stats_out, next_out)


def solution(mesh):
    placed = (
        P("dp", "feat"),
        P("dp", None),
        P("feat", None),
        P("feat", "dp", None, None, None),
        P(),
        P("dp", "feat"),
    )
    return jax.shard_map(
        body,
        mesh=mesh,
        in_specs=placed,
        out_specs=(P("feat", None), P("feat", "dp", None, None, None), P("dp", "feat")),
        check_vma=False,
    )
```

profile of v0, /device:TPU:0, one launch (start us, length us, event | category | flops | bytes accessed | tf_op | source)
XLA Modules:
  0.0 700.2 jit_solution(15082206161460627291)
XLA Ops:
  13.1 5.7 fusion.363
  18.9 328.1 %all-reduce.5 = bf16[2048,1024]{1,0:T(8,128)(2,1)} all-reduce(f32[2048,1024]{1,0:T(8,128)} %fusion.363), channel_id=1, replica_groups=mesh['dp'=8,'feat'=4] {'dp'}, use_global_device_ids=true, to_apply=%region_2.3 | all-reduce | flops 2097152 | bytes 12582912 | tf_op jit(solution)/shard_map/psum | solution.py:64
  347.0 1.8 multiply_reduce_fusion
  351.3 1.0 convolution_convert_fusion.12
  354.6 1.9 multiply_reduce_fusion.1
  358.9 1.0 convolution_convert_fusion.27
  363.3 1.9 multiply_reduce_fusion.2
  367.6 1.0 convolution_convert_fusion.42
  370.9 1.8 multiply_reduce_fusion.3
  375.2 1.0 convolution_convert_fusion.57
  421.7 1.2 convolution_convert_fusion.6
  425.8 1.2 fusion.2
  427.4 1.2 fusion.6
  431.4 1.2 fusion.10
  435.5 1.2 fusion.14
  477.7 1.0 fusion.78
  478.8 1.1 fusion.87
  479.8 1.1 fusion.96
  481.2 166.1 %all-reduce.4.cloned.1.call-done = (bf16[1,256,256]{2,1,0:T(8,128)(2,1)}, bf16[1,256,256]{2,1,0:T(8,128)(2,1)}, bf16[1,256,256]{2,1,0:T(8,128)(2,1)}, bf16[1,256...) async-done(((bf16[1,256,256]{2,1,0:T(8,128)(2,1)}, ...) | async-done | bytes 4194320 | tf_op jit(solution)/shard_map/psum | solution.py:13
  647.4 1.1 constant_dynamic-update-slice_fusion.31
  648.5 0.9 constant_dynamic-update-slice_fusion.30
  649.4 0.9 constant_dynamic-update-slice_fusion.29
  651.3 0.9 constant_dynamic-update-slice_fusion.27
  652.2 0.9 constant_dynamic-update-slice_fusion.26
  662.7 3.2 copy.15
  666.0 1.0 copy.18
  667.1 1.9 copy-done.2
  669.0 2.1 fusion
  671.2 1.0 maximum_bitcast_fusion
  672.2 6.6 reshape.195
  678.8 12.9 %reduce-scatter.2.cloned.1.call-done = bf16[256,256]{0,1:T(8,128)(2,1)} async-done(((bf16[256,1024]{0,1:T(8,128)(2,1)}), bf16[256,256]{0,1:T(8,128)(2,1)}) %reduce-scatter.2.cloned.1.call-update) | async-done | bytes 131088 | tf_op jit(solution)/shard_map/reduce_scatter | solution.py:113
  691.7 1.7 copy.16
  (148 shorter events, 36.2 us)
Async XLA Ops:
  7.2 6.0 copy-start
  7.2 640.1 %all-reduce.4.cloned.1.call-start = ((), (), s32[]{:S(2)}) async-start(), calls=%async_computation.2 | async-start | bytes 8388608 | tf_op jit(solution)/shard_map/psum | solution.py:13
  18.9 328.1 %copy-start.3 = (f32[1,1,4,256,256]{4,3,2,1,0:T(8,128)S(1)}, f32[1,1,4,256,256]{4,3,2,1,0:T(8,128)}, u32[]{:S(2)}) copy-start(f32[1,1,4,256,256]{4,3,2,1,0:T(8,128)} %param.9) | copy-start | bytes 3145732
  419.8 5.3 copy-start.21
  425.4 5.3 copy-start.22
  429.4 5.3 copy-start.23
  480.9 210.8 %reduce-scatter.2.cloned.1.call-start = ((), (), s32[]{:S(2)}) async-start(), calls=%async_computation.1 | async-start | bytes 655360 | tf_op jit(solution)/shard_map/reduce_scatter | solution.py:113
  647.3 15.0 %copy-start.19 = (bf16[1,256,256]{2,1,0:T(8,128)(2,1)S(1)}, bf16[1,256,256]{2,1,0:T(8,128)(2,1)}, u32[]{:S(2)}) copy-start(bf16[1,256,256]{2,1,0:T(8,128)(2,1)} %get-tuple-element.25) | copy-start | bytes 393220
  647.3 15.0 %copy-start.18 = (bf16[1,256,256]{2,1,0:T(8,128)(2,1)S(1)}, bf16[1,256,256]{2,1,0:T(8,128)(2,1)}, u32[]{:S(2)}) copy-start(bf16[1,256,256]{2,1,0:T(8,128)(2,1)} %get-tuple-element.26) | copy-start | bytes 393220
  647.3 15.0 %copy-start.17 = (bf16[1,256,256]{2,1,0:T(8,128)(2,1)S(1)}, bf16[1,256,256]{2,1,0:T(8,128)(2,1)}, u32[]{:S(2)}) copy-start(bf16[1,256,256]{2,1,0:T(8,128)(2,1)} %get-tuple-element.27) | copy-start | bytes 393220
  647.3 15.0 %copy-start.16 = (bf16[1,256,256]{2,1,0:T(8,128)(2,1)S(1)}, bf16[1,256,256]{2,1,0:T(8,128)(2,1)}, u32[]{:S(2)}) copy-start(bf16[1,256,256]{2,1,0:T(8,128)(2,1)} %get-tuple-element.28) | copy-start | bytes 393220
  647.3 15.1 %copy-start.15 = (bf16[1,256,256]{2,1,0:T(8,128)(2,1)S(1)}, bf16[1,256,256]{2,1,0:T(8,128)(2,1)}, u32[]{:S(2)}) copy-start(bf16[1,256,256]{2,1,0:T(8,128)(2,1)} %get-tuple-element.29) | copy-start | bytes 393220
  647.3 15.1 %copy-start.14 = (bf16[1,256,256]{2,1,0:T(8,128)(2,1)S(1)}, bf16[1,256,256]{2,1,0:T(8,128)(2,1)}, u32[]{:S(2)}) copy-start(bf16[1,256,256]{2,1,0:T(8,128)(2,1)} %get-tuple-element.30) | copy-start | bytes 393220
  647.3 15.1 %copy-start.13 = (bf16[1,256,256]{2,1,0:T(8,128)(2,1)S(1)}, bf16[1,256,256]{2,1,0:T(8,128)(2,1)}, u32[]{:S(2)}) copy-start(bf16[1,256,256]{2,1,0:T(8,128)(2,1)} %get-tuple-element.31) | copy-start | bytes 393220
  647.3 15.1 %copy-start.12 = (bf16[1,256,256]{2,1,0:T(8,128)(2,1)S(1)}, bf16[1,256,256]{2,1,0:T(8,128)(2,1)}, u32[]{:S(2)}) copy-start(bf16[1,256,256]{2,1,0:T(8,128)(2,1)} %get-tuple-element.32) | copy-start | bytes 393220
  647.4 15.2 %copy-start.11 = (bf16[1,256,256]{2,1,0:T(8,128)(2,1)S(1)}, bf16[1,256,256]{2,1,0:T(8,128)(2,1)}, u32[]{:S(2)}) copy-start(bf16[1,256,256]{2,1,0:T(8,128)(2,1)} %get-tuple-element.33) | copy-start | bytes 393220
  647.4 15.2 %copy-start.10 = (bf16[1,256,256]{2,1,0:T(8,128)(2,1)S(1)}, bf16[1,256,256]{2,1,0:T(8,128)(2,1)}, u32[]{:S(2)}) copy-start(bf16[1,256,256]{2,1,0:T(8,128)(2,1)} %get-tuple-element.34) | copy-start | bytes 393220
  647.4 15.2 %copy-start.9 = (bf16[1,256,256]{2,1,0:T(8,128)(2,1)S(1)}, bf16[1,256,256]{2,1,0:T(8,128)(2,1)}, u32[]{:S(2)}) copy-start(bf16[1,256,256]{2,1,0:T(8,128)(2,1)} %get-tuple-element.35) | copy-start | bytes 393220
  647.4 15.2 %copy-start.8 = (bf16[1,256,256]{2,1,0:T(8,128)(2,1)S(1)}, bf16[1,256,256]{2,1,0:T(8,128)(2,1)}, u32[]{:S(2)}) copy-start(bf16[1,256,256]{2,1,0:T(8,128)(2,1)} %get-tuple-element.36) | copy-start | bytes 393220
  647.4 15.2 %copy-start.7 = (bf16[1,256,256]{2,1,0:T(8,128)(2,1)S(1)}, bf16[1,256,256]{2,1,0:T(8,128)(2,1)}, u32[]{:S(2)}) copy-start(bf16[1,256,256]{2,1,0:T(8,128)(2,1)} %get-tuple-element.37) | copy-start | bytes 393220
  647.4 15.2 %copy-start.6 = (bf16[1,256,256]{2,1,0:T(8,128)(2,1)S(1)}, bf16[1,256,256]{2,1,0:T(8,128)(2,1)}, u32[]{:S(2)}) copy-start(bf16[1,256,256]{2,1,0:T(8,128)(2,1)} %get-tuple-element.38) | copy-start | bytes 393220
  647.4 15.3 %copy-start.5 = (bf16[1,256,256]{2,1,0:T(8,128)(2,1)S(1)}, bf16[1,256,256]{2,1,0:T(8,128)(2,1)}, u32[]{:S(2)}) copy-start(bf16[1,256,256]{2,1,0:T(8,128)(2,1)} %get-tuple-element.39) | copy-start | bytes 393220
  647.4 15.3 %copy-start.4 = (bf16[1,256,256]{2,1,0:T(8,128)(2,1)S(1)}, bf16[1,256,256]{2,1,0:T(8,128)(2,1)}, u32[]{:S(2)}) copy-start(bf16[1,256,256]{2,1,0:T(8,128)(2,1)} %get-tuple-element.40) | copy-start | bytes 393220
  666.0 3.0 copy-start.20
  667.0 1.9 copy-start.2
  671.1 22.2 %copy-start.1 = (bf16[256,2048]{1,0:T(8,128)(2,1)S(1)}, bf16[256,2048]{1,0:T(8,128)(2,1)}, u32[]{:S(2)}) copy-start(bf16[256,2048]{1,0:T(8,128)(2,1)} %param.6) | copy-start | bytes 3145732
Sparse Core Ops, SparseCore 0:
  481.0 166.2 all-reduce.3
  671.3 20.4 reduce-scatter.1
where the time goes:
time: 702 us; the launch traced here: 700 us
  blocking collectives  328 us (47%)
  waiting for transfers between devices  179 us (25%)
  between operations  108 us (15%)
  matrix products  40.3 us (6%)
  local copies, waits for them, and re-layouts  27 us (4%)
  other arithmetic  17.4 us (2%)
    psum x1, blocking collectives, body(): summed = lax.psum(partial_grad, 'dp')  328 us
    psum x1, waiting for transfers between devices, from_root(): return lax.psum(jnp.where(mine, x, jnp.zeros_like(x)), axis)  166 us
    unnamed x82, local copies, waits for them, and re-layouts  19.8 us
  transfers between devices with their start and end apart: 2, of which 2 were waited for; matrix products, arithmetic and copies ran while one was open for 1% of the time, Pallas kernels for 0%

commit v1 on v0

--- a/solution.py
+++ b/solution.py
@@ -10,7 +10,7 @@
 
 def from_root(x, axis, root):
     mine = lax.axis_index(axis) == root
-    return lax.psum(jnp.where(mine, x, jnp.zeros_like(x)), axis)
+    return jnp.sum(lax.all_gather(jnp.where(mine, x, jnp.zeros_like(x)), axis), axis=0)
 
 
 def newton_root(stats):

time: 702 us -> 1780 us (2.54)
  waiting for transfers between devices: 179 us -> 1190 us
  other arithmetic: 17.4 us -> 54.7 us
  local copies, waits for them, and re-layouts: 27 us -> 47.5 us
    all_gather x0 -> x32, waiting for transfers between devices: none -> 1160 us  [from_root(): lax.all_gather(jnp.where(mine, x, jnp.zeros_like(x)), axis)]
    psum x1 -> x0, waiting for transfers between devices: 166 us -> none  [from_root(): return lax.psum(jnp.where(mine, x, jnp.zeros_like(x)), axis)]
    reduce_sum x0 -> x32, other arithmetic: none -> 43.9 us  [from_root(): jnp.sum(lax.all_gather(jnp.where(mine, x, jnp.zeros_like(x)), axis), axis=0)]
  transfers between devices with their start and end apart: 2 -> 33, of which waited for: 2 -> 31; matrix products, arithmetic and copies ran while one was open for 1% -> 4% of each run, Pallas kernels for 0% -> 0%
where the time goes in v1:
time: 1780 us; the launch traced here: 1770 us
  waiting for transfers between devices  1190 us (67%)
  blocking collectives  328 us (18%)
  between operations  110 us (6%)
  other arithmetic  54.7 us (3%)
  local copies, waits for them, and re-layouts  47.5 us (3%)
  matrix products  43.7 us (2%)
    all_gather x32, waiting for transfers between devices, from_root(): lax.all_gather(jnp.where(mine, x, jnp.zeros_like(x)), axis)  1160 us
    psum x1, blocking collectives, body(): summed = lax.psum(partial_grad, 'dp')  328 us
    reduce_sum x32, other arithmetic, from_root(): jnp.sum(lax.all_gather(jnp.where(mine, x, jnp.zeros_like(x)), axis), axis=0)  43.9 us
  transfers between devices with their start and end apart: 33, of which 31 were waited for; matrix products, arithmetic and copies ran while one was open for 4% of the time, Pallas kernels for 0%

profile of v1, /device:TPU:0, one launch (start us, length us, event | category | flops | bytes accessed | tf_op | source)
XLA Modules:
  0.0 1773.1 jit_solution(9728453864608357082)
XLA Ops:
  18.9 328.1 %all-reduce.1 = bf16[2048,1024]{1,0:T(8,128)(2,1)} all-reduce(f32[2048,1024]{1,0:T(8,128)} %fusion.363), channel_id=1, replica_groups=mesh['dp'=8,'feat'=4] {'dp'}, use_global_device_ids=true, to_apply=%region_2.3 | all-reduce | flops 2097152 | bytes 12582912 | tf_op jit(solution)/shard_map/psum | solution.py:64
  509.4 24.8 %all-gather.37.cloned.1.call-done = bf16[8,256,256]{2,1,0:T(8,128)(2,1)} async-done(((bf16[1,256,256]{2,1,0:T(8,128)(2,1)}), bf16[8,256,256]{2,1,0:T(8,128)(2,1)}) %all-gather.37.cloned.1.call-update) | async-done | bytes 1048592 | tf_op jit(solution)/shard_map/all_gather | solution.py:13
  536.3 39.5 %all-gather.39.cloned.1.call-done = bf16[8,256,256]{2,1,0:T(8,128)(2,1)} async-done(((bf16[1,256,256]{2,1,0:T(8,128)(2,1)}), bf16[8,256,256]{2,1,0:T(8,128)(2,1)}) %all-gather.39.cloned.1.call-update) | async-done | bytes 1048592 | tf_op jit(solution)/shard_map/all_gather | solution.py:13
  577.8 39.5 %all-gather.41.cloned.1.call-done = bf16[8,256,256]{2,1,0:T(8,128)(2,1)} async-done(((bf16[1,256,256]{2,1,0:T(8,128)(2,1)}), bf16[8,256,256]{2,1,0:T(8,128)(2,1)}) %all-gather.41.cloned.1.call-update) | async-done | bytes 1048592 | tf_op jit(solution)/shard_map/all_gather | solution.py:13
  619.4 39.0 %all-gather.43.cloned.1.call-done = bf16[8,256,256]{2,1,0:T(8,128)(2,1)} async-done(((bf16[1,256,256]{2,1,0:T(8,128)(2,1)}), bf16[8,256,256]{2,1,0:T(8,128)(2,1)}) %all-gather.43.cloned.1.call-update) | async-done | bytes 1048592 | tf_op jit(solution)/shard_map/all_gather | solution.py:13
  660.4 39.1 %all-gather.45.cloned.1.call-done = bf16[8,256,256]{2,1,0:T(8,128)(2,1)} async-done(((bf16[1,256,256]{2,1,0:T(8,128)(2,1)}), bf16[8,256,256]{2,1,0:T(8,128)(2,1)}) %all-gather.45.cloned.1.call-update) | async-done | bytes 1048592 | tf_op jit(solution)/shard_map/all_gather | solution.py:13
  701.5 39.1 %all-gather.47.cloned.1.call-done = bf16[8,256,256]{2,1,0:T(8,128)(2,1)} async-done(((bf16[1,256,256]{2,1,0:T(8,128)(2,1)}), bf16[8,256,256]{2,1,0:T(8,128)(2,1)}) %all-gather.47.cloned.1.call-update) | async-done | bytes 1048592 | tf_op jit(solution)/shard_map/all_gather | solution.py:13
  742.7 39.1 %all-gather.49.cloned.1.call-done = bf16[8,256,256]{2,1,0:T(8,128)(2,1)} async-done(((bf16[1,256,256]{2,1,0:T(8,128)(2,1)}), bf16[8,256,256]{2,1,0:T(8,128)(2,1)}) %all-gather.49.cloned.1.call-update) | async-done | bytes 1048592 | tf_op jit(solution)/shard_map/all_gather | solution.py:13
  783.8 39.0 %all-gather.51.cloned.1.call-done = bf16[8,256,256]{2,1,0:T(8,128)(2,1)} async-done(((bf16[1,256,256]{2,1,0:T(8,128)(2,1)}), bf16[8,256,256]{2,1,0:T(8,128)(2,1)}) %all-gather.51.cloned.1.call-update) | async-done | bytes 1048592 | tf_op jit(solution)/shard_map/all_gather | solution.py:13
  824.8 39.1 %all-gather.53.cloned.1.call-done = bf16[8,256,256]{2,1,0:T(8,128)(2,1)} async-done(((bf16[1,256,256]{2,1,0:T(8,128)(2,1)}), bf16[8,256,256]{2,1,0:T(8,128)(2,1)}) %all-gather.53.cloned.1.call-update) | async-done | bytes 1048592 | tf_op jit(solution)/shard_map/all_gather | solution.py:13
  866.0 39.0 %all-gather.55.cloned.1.call-done = bf16[8,256,256]{2,1,0:T(8,128)(2,1)} async-done(((bf16[1,256,256]{2,1,0:T(8,128)(2,1)}), bf16[8,256,256]{2,1,0:T(8,128)(2,1)}) %all-gather.55.cloned.1.call-update) | async-done | bytes 1048592 | tf_op jit(solution)/shard_map/all_gather | solution.py:13
  907.0 39.1 %all-gather.57.cloned.1.call-done = bf16[8,256,256]{2,1,0:T(8,128)(2,1)} async-done(((bf16[1,256,256]{2,1,0:T(8,128)(2,1)}), bf16[8,256,256]{2,1,0:T(8,128)(2,1)}) %all-gather.57.cloned.1.call-update) | async-done | bytes 1048592 | tf_op jit(solution)/shard_map/all_gather | solution.py:13
  948.1 39.0 %all-gather.59.cloned.1.call-done = bf16[8,256,256]{2,1,0:T(8,128)(2,1)} async-done(((bf16[1,256,256]{2,1,0:T(8,128)(2,1)}), bf16[8,256,256]{2,1,0:T(8,128)(2,1)}) %all-gather.59.cloned.1.call-update) | async-done | bytes 1048592 | tf_op jit(solution)/shard_map/all_gather | solution.py:13
  989.1 39.0 %all-gather.61.cloned.1.call-done = bf16[8,256,256]{2,1,0:T(8,128)(2,1)} async-done(((bf16[1,256,256]{2,1,0:T(8,128)(2,1)}), bf16[8,256,256]{2,1,0:T(8,128)(2,1)}) %all-gather.61.cloned.1.call-update) | async-done | bytes 1048592 | tf_op jit(solution)/shard_map/all_gather | solution.py:13
  1030.1 39.0 %all-gather.63.cloned.1.call-done = bf16[8,256,256]{2,1,0:T(8,128)(2,1)} async-done(((bf16[1,256,256]{2,1,0:T(8,128)(2,1)}), bf16[8,256,256]{2,1,0:T(8,128)(2,1)}) %all-gather.63.cloned.1.call-update) | async-done | bytes 1048592 | tf_op jit(solution)/shard_map/all_gather | solution.py:13
  1071.1 39.0 %all-gather.65.cloned.1.call-done = bf16[8,256,256]{2,1,0:T(8,128)(2,1)} async-done(((bf16[1,256,256]{2,1,0:T(8,128)(2,1)}), bf16[8,256,256]{2,1,0:T(8,128)(2,1)}) %all-gather.65.cloned.1.call-update) | async-done | bytes 1048592 | tf_op jit(solution)/shard_map/all_gather | solution.py:13
  1112.1 39.0 %all-gather.67.cloned.1.call-done = bf16[8,256,256]{2,1,0:T(8,128)(2,1)} async-done(((bf16[1,256,256]{2,1,0:T(8,128)(2,1)}), bf16[8,256,256]{2,1,0:T(8,128)(2,1)}) %all-gather.67.cloned.1.call-update) | async-done | bytes 1048592 | tf_op jit(solution)/shard_map/all_gather | solution.py:13
  1153.1 39.1 %all-gather.69.cloned.1.call-done = bf16[8,256,256]{2,1,0:T(8,128)(2,1)} async-done(((bf16[1,256,256]{2,1,0:T(8,128)(2,1)}), bf16[8,256,256]{2,1,0:T(8,128)(2,1)}) %all-gather.69.cloned.1.call-update) | async-done | bytes 1048592 | tf_op jit(solution)/shard_map/all_gather | solution.py:13
  1194.3 39.0 %all-gather.71.cloned.1.call-done = bf16[8,256,256]{2,1,0:T(8,128)(2,1)} async-done(((bf16[1,256,256]{2,1,0:T(8,128)(2,1)}), bf16[8,256,256]{2,1,0:T(8,128)(2,1)}) %all-gather.71.cloned.1.call-update) | async-done | bytes 1048592 | tf_op jit(solution)/shard_map/all_gather | solution.py:13
  1235.3 39.1 %all-gather.73.cloned.1.call-done = bf16[8,256,256]{2,1,0:T(8,128)(2,1)} async-done(((bf16[1,256,256]{2,1,0:T(8,128)(2,1)}), bf16[8,256,256]{2,1,0:T(8,128)(2,1)}) %all-gather.73.cloned.1.call-update) | async-done | bytes 1048592 | tf_op jit(solution)/shard_map/all_gather | solution.py:13
  1276.4 39.1 %all-gather.75.cloned.1.call-done = bf16[8,256,256]{2,1,0:T(8,128)(2,1)} async-done(((bf16[1,256,256]{2,1,0:T(8,128)(2,1)}), bf16[8,256,256]{2,1,0:T(8,128)(2,1)}) %all-gather.75.cloned.1.call-update) | async-done | bytes 1048592 | tf_op jit(solution)/shard_map/all_gather | solution.py:13
  1317.6 39.1 %all-gather.77.cloned.1.call-done = bf16[8,256,256]{2,1,0:T(8,128)(2,1)} async-done(((bf16[1,256,256]{2,1,0:T(8,128)(2,1)}), bf16[8,256,256]{2,1,0:T(8,128)(2,1)}) %all-gather.77.cloned.1.call-update) | async-done | bytes 1048592 | tf_op jit(solution)/shard_map/all_gather | solution.py:13
  1358.7 39.0 %all-gather.79.cloned.1.call-done = bf16[8,256,256]{2,1,0:T(8,128)(2,1)} async-done(((bf16[1,256,256]{2,1,0:T(8,128)(2,1)}), bf16[8,256,256]{2,1,0:T(8,128)(2,1)}) %all-gather.79.cloned.1.call-update) | async-done | bytes 1048592 | tf_op jit(solution)/shard_map/all_gather | solution.py:13
  1399.1 39.8 %all-gather.81.cloned.1.call-done = bf16[8,256,256]{2,1,0:T(8,128)(2,1)} async-done(((bf16[1,256,256]{2,1,0:T(8,128)(2,1)}), bf16[8,256,256]{2,1,0:T(8,128)(2,1)}) %all-gather.81.cloned.1.call-update) | async-done | bytes 1048592 | tf_op jit(solution)/shard_map/all_gather | solution.py:13
  1440.2 39.6 %all-gather.83.cloned.1.call-done = bf16[8,256,256]{2,1,0:T(8,128)(2,1)} async-done(((bf16[1,256,256]{2,1,0:T(8,128)(2,1)}), bf16[8,256,256]{2,1,0:T(8,128)(2,1)}) %all-gather.83.cloned.1.call-update) | async-done | bytes 1048592 | tf_op jit(solution)/shard_map/all_gather | solution.py:13
  1481.2 39.6 %all-gather.85.cloned.1.call-done = bf16[8,256,256]{2,1,0:T(8,128)(2,1)} async-done(((bf16[1,256,256]{2,1,0:T(8,128)(2,1)}), bf16[8,256,256]{2,1,0:T(8,128)(2,1)}) %all-gather.85.cloned.1.call-update) | async-done | bytes 1048592 | tf_op jit(solution)/shard_map/all_gather | solution.py:13
  1522.2 39.8 %all-gather.87.cloned.1.call-done = bf16[8,256,256]{2,1,0:T(8,128)(2,1)} async-done(((bf16[1,256,256]{2,1,0:T(8,128)(2,1)}), bf16[8,256,256]{2,1,0:T(8,128)(2,1)}) %all-gather.87.cloned.1.call-update) | async-done | bytes 1048592 | tf_op jit(solution)/shard_map/all_gather | solution.py:13
  1563.3 39.8 %all-gather.89.cloned.1.call-done = bf16[8,256,256]{2,1,0:T(8,128)(2,1)} async-done(((bf16[1,256,256]{2,1,0:T(8,128)(2,1)}), bf16[8,256,256]{2,1,0:T(8,128)(2,1)}) %all-gather.89.cloned.1.call-update) | async-done | bytes 1048592 | tf_op jit(solution)/shard_map/all_gather | solution.py:13
  1604.5 39.6 %all-gather.91.cloned.1.call-done = bf16[8,256,256]{2,1,0:T(8,128)(2,1)} async-done(((bf16[1,256,256]{2,1,0:T(8,128)(2,1)}), bf16[8,256,256]{2,1,0:T(8,128)(2,1)}) %all-gather.91.cloned.1.call-update) | async-done | bytes 1048592 | tf_op jit(solution)/shard_map/all_gather | solution.py:13
  1645.5 39.8 %all-gather.93.cloned.1.call-done = bf16[8,256,256]{2,1,0:T(8,128)(2,1)} async-done(((bf16[1,256,256]{2,1,0:T(8,128)(2,1)}), bf16[8,256,256]{2,1,0:T(8,128)(2,1)}) %all-gather.93.cloned.1.call-update) | async-done | bytes 1048592 | tf_op jit(solution)/shard_map/all_gather | solution.py:13
  1692.0 34.5 %all-gather.95.cloned.1.call-done = bf16[8,256,256]{2,1,0:T(8,128)(2,1)} async-done(((bf16[1,256,256]{2,1,0:T(8,128)(2,1)}), bf16[8,256,256]{2,1,0:T(8,128)(2,1)}) %all-gather.95.cloned.1.call-update) | async-done | bytes 1048592 | tf_op jit(solution)/shard_map/all_gather | solution.py:13
  1752.0 12.6 reduce-scatter.2.cloned.1.call-done
  (237 shorter events, 164.6 us)
Async XLA Ops:
  7.2 498.2 %all-gather.33.cloned.1.call-start = ((), (), s32[]{:S(2)}) async-start(), calls=%async_computation.1 | async-start | bytes 1179648 | tf_op jit(solution)/shard_map/all_gather | solution.py:13
  413.9 120.3 %all-gather.37.cloned.1.call-start = ((), (), s32[]{:S(2)}) async-start(), calls=%async_computation.3 | async-start | bytes 1179648 | tf_op jit(solution)/shard_map/all_gather | solution.py:13
  414.6 161.2 %all-gather.39.cloned.1.call-start = ((), (), s32[]{:S(2)}) async-start(), calls=%async_computation.4 | async-start | bytes 1179648 | tf_op jit(solution)/shard_map/all_gather | solution.py:13
  415.2 202.2 %all-gather.41.cloned.1.call-start = ((), (), s32[]{:S(2)}) async-start(), calls=%async_computation.5 | async-start | bytes 1179648 | tf_op jit(solution)/shard_map/all_gather | solution.py:13
  415.8 242.6 %all-gather.43.cloned.1.call-start = ((), (), s32[]{:S(2)}) async-start(), calls=%async_computation.6 | async-start | bytes 1179648 | tf_op jit(solution)/shard_map/all_gather | solution.py:13
  441.0 258.5 %all-gather.45.cloned.1.call-start = ((), (), s32[]{:S(2)}) async-start(), calls=%async_computation.7 | async-start | bytes 1179648 | tf_op jit(solution)/shard_map/all_gather | solution.py:13
  441.8 298.9 %all-gather.47.cloned.1.call-start = ((), (), s32[]{:S(2)}) async-start(), calls=%async_computation.8 | async-start | bytes 1179648 | tf_op jit(solution)/shard_map/all_gather | solution.py:13
  442.5 339.3 %all-gather.49.cloned.1.call-start = ((), (), s32[]{:S(2)}) async-start(), calls=%async_computation.9 | async-start | bytes 1179648 | tf_op jit(solution)/shard_map/all_gather | solution.py:13
  443.2 379.6 %all-gather.51.cloned.1.call-start = ((), (), s32[]{:S(2)}) async-start(), calls=%async_computation.10 | async-start | bytes 1179648 | tf_op jit(solution)/shard_map/all_gather | solution.py:13
  443.8 420.1 %all-gather.53.cloned.1.call-start = ((), (), s32[]{:S(2)}) async-start(), calls=%async_computation.11 | async-start | bytes 1179648 | tf_op jit(solution)/shard_map/all_gather | solution.py:13
  444.6 460.4 %all-gather.55.cloned.1.call-start = ((), (), s32[]{:S(2)}) async-start(), calls=%async_computation.12 | async-start | bytes 1179648 | tf_op jit(solution)/shard_map/all_gather | solution.py:13
  445.1 501.0 %all-gather.57.cloned.1.call-start = ((), (), s32[]{:S(2)}) async-start(), calls=%async_computation.13 | async-start | bytes 1179648 | tf_op jit(solution)/shard_map/all_gather | solution.py:13
  445.9 541.2 %all-gather.59.cloned.1.call-start = ((), (), s32[]{:S(2)}) async-start(), calls=%async_computation.14 | async-start | bytes 1179648 | tf_op jit(solution)/shard_map/all_gather | solution.py:13
  446.5 581.6 %all-gather.61.cloned.1.call-start = ((), (), s32[]{:S(2)}) async-start(), calls=%async_computation.15 | async-start | bytes 1179648 | tf_op jit(solution)/shard_map/all_gather | solution.py:13
  470.3 598.8 %all-gather.63.cloned.1.call-start = ((), (), s32[]{:S(2)}) async-start(), calls=%async_computation.16 | async-start | bytes 1179648 | tf_op jit(solution)/shard_map/all_gather | solution.py:13
  470.9 639.2 %all-gather.65.cloned.1.call-start = ((), (), s32[]{:S(2)}) async-start(), calls=%async_computation.17 | async-start | bytes 1179648 | tf_op jit(solution)/shard_map/all_gather | solution.py:13
  471.5 679.6 %all-gather.67.cloned.1.call-start = ((), (), s32[]{:S(2)}) async-start(), calls=%async_computation.18 | async-start | bytes 1179648 | tf_op jit(solution)/shard_map/all_gather | solution.py:13
  472.1 720.2 %all-gather.69.cloned.1.call-start = ((), (), s32[]{:S(2)}) async-start(), calls=%async_computation.19 | async-start | bytes 1179648 | tf_op jit(solution)/shard_map/all_gather | solution.py:13
  472.8 760.4 %all-gather.71.cloned.1.call-start = ((), (), s32[]{:S(2)}) async-start(), calls=%async_computation.20 | async-start | bytes 1179648 | tf_op jit(solution)/shard_map/all_gather | solution.py:13
  473.4 801.0 %all-gather.73.cloned.1.call-start = ((), (), s32[]{:S(2)}) async-start(), calls=%async_computation.21 | async-start | bytes 1179648 | tf_op jit(solution)/shard_map/all_gather | solution.py:13
  474.1 841.4 %all-gather.75.cloned.1.call-start = ((), (), s32[]{:S(2)}) async-start(), calls=%async_computation.22 | async-start | bytes 1179648 | tf_op jit(solution)/shard_map/all_gather | solution.py:13
  474.9 881.8 %all-gather.77.cloned.1.call-start = ((), (), s32[]{:S(2)}) async-start(), calls=%async_computation.23 | async-start | bytes 1179648 | tf_op jit(solution)/shard_map/all_gather | solution.py:13
  475.6 922.1 %all-gather.79.cloned.1.call-start = ((), (), s32[]{:S(2)}) async-start(), calls=%async_computation.24 | async-start | bytes 1179648 | tf_op jit(solution)/shard_map/all_gather | solution.py:13
  499.8 939.0 %all-gather.81.cloned.1.call-start = ((), (), s32[]{:S(2)}) async-start(), calls=%async_computation.25 | async-start | bytes 1179648 | tf_op jit(solution)/shard_map/all_gather | solution.py:13
  500.6 979.3 %all-gather.83.cloned.1.call-start = ((), (), s32[]{:S(2)}) async-start(), calls=%async_computation.26 | async-start | bytes 1179648 | tf_op jit(solution)/shard_map/all_gather | solution.py:13
  501.1 1019.7 %all-gather.85.cloned.1.call-start = ((), (), s32[]{:S(2)}) async-start(), calls=%async_computation.27 | async-start | bytes 1179648 | tf_op jit(solution)/shard_map/all_gather | solution.py:13
  501.7 1060.2 %all-gather.87.cloned.1.call-start = ((), (), s32[]{:S(2)}) async-start(), calls=%async_computation.28 | async-start | bytes 1179648 | tf_op jit(solution)/shard_map/all_gather | solution.py:13
  502.5 1100.6 %all-gather.89.cloned.1.call-start = ((), (), s32[]{:S(2)}) async-start(), calls=%async_computation.29 | async-start | bytes 1179648 | tf_op jit(solution)/shard_map/all_gather | solution.py:13
  503.2 1140.9 %all-gather.91.cloned.1.call-start = ((), (), s32[]{:S(2)}) async-start(), calls=%async_computation.30 | async-start | bytes 1179648 | tf_op jit(solution)/shard_map/all_gather | solution.py:13
  503.8 1181.5 %all-gather.93.cloned.1.call-start = ((), (), s32[]{:S(2)}) async-start(), calls=%async_computation.31 | async-start | bytes 1179648 | tf_op jit(solution)/shard_map/all_gather | solution.py:13
  504.5 1221.9 %all-gather.95.cloned.1.call-start = ((), (), s32[]{:S(2)}) async-start(), calls=%async_computation.32 | async-start | bytes 1179648 | tf_op jit(solution)/shard_map/all_gather | solution.py:13
  505.3 1259.4 %reduce-scatter.2.cloned.1.call-start = ((), (), s32[]{:S(2)}) async-start(), calls=%async_computation.33 | async-start | bytes 655360 | tf_op jit(solution)/shard_map/reduce_scatter | solution.py:113
  (7 other events, 464.4 us)
Sparse Core Ops, SparseCore 0:
  413.2 38.6 all-gather.32
  454.0 39.0 all-gather.34
  495.2 38.9 all-gather.36
  536.8 38.9 all-gather.38
  578.3 38.9 all-gather.40
  619.3 38.9 all-gather.42
  660.5 38.9 all-gather.44
  701.6 38.9 all-gather.46
  742.8 38.9 all-gather.48
  783.8 38.9 all-gather.50
  824.9 38.9 all-gather.52
  865.9 38.9 all-gather.54
  907.1 38.9 all-gather.56
  948.1 38.9 all-gather.58
  989.1 38.9 all-gather.60
  1030.1 38.9 all-gather.62
  1071.1 38.9 all-gather.64
  1112.1 38.9 all-gather.66
  1153.2 38.9 all-gather.68
  1194.2 38.9 all-gather.70
  1235.4 38.9 all-gather.72
  1276.5 38.9 all-gather.74
  1317.7 38.9 all-gather.76
  1358.7 38.9 all-gather.78
  1399.8 38.9 all-gather.80
  1440.8 38.9 all-gather.82
  1481.8 38.9 all-gather.84
  1522.9 38.9 all-gather.86
  1564.1 38.9 all-gather.88
  1605.1 38.9 all-gather.90
  1646.2 38.9 all-gather.92
  1687.4 38.9 all-gather.94
  (1 shorter events, 20.3 us)
